TPU v7x, 32 devices: a whole 2x2x4 slice. The times are simulated.
32 devices in a mesh: row: 4 (over z), col: 8 (over y, x, core).
Axes of the slice: x: 2, y: 2, z: 4, core: 2. Of those that a mesh axis runs over, the one named last changes fastest.
Arguments:
- eigvecs: bfloat16 [40960, 2048], P('row', 'col'), may hold values from -0.125 to 0.125
- reflectors: bfloat16 [2, 40960, 128], P(None, 'row'), may hold values from -6 to 6
- factors: float32 [2, 128, 128], replicated, may hold values from -0.00024414062 to 0.00024414062
- frequencies: float32 [2048], replicated, may hold values from 0.3 to 3
- region_blocks: int32 [72], P('row'), may hold values from 0 to 319, as said below
Outputs:
- covariance: float32 [9216, 9216], P('row', 'col')
Inputs may be any that keep to these rules, and one draw needn't show every extreme that they name: `region_blocks`: the 72 block numbers are distinct and ascending; exactly 18 of them lie in each consecutive run of 80 block numbers.
All inputs are finite; a program needn't handle non-finite values.
Results may differ from a plain program's by a relative error of at most 0.004.
Values may be sent and summed in bfloat16 or wider, within the bound.
A program may use at most 128 MiB of HBM per device.

v0:
```python
import jax
import jax.numpy as jnp
from jax import lax
from jax.sharding import PartitionSpec as P

BLOCK = 128


def contract_rows(left, right):
    return lax.dot_general(
        left, right, (((0,), (0,)), ((), ())), preferred_element_type=jnp.float32
    )


def contract_cols(left, right):
    return lax.dot_general(
        left, right, (((1,), (1,)), ((), ())), preferred_element_type=jnp.float32
    )


def per_device(eigvecs, reflectors, factors, frequencies, region_blocks):
    highest = lax.Precision.HIGHEST
    first_block = reflectors[0]
    second_block = reflectors[1]
    first_factor = jnp.triu(factors[0])
    second_factor = jnp.triu(factors[1])
    second_local = contract_rows(second_block, eigvecs)
    first_local = contract_rows(first_block, eigvecs)
    cross_local = contract_rows(first_block, second_block)
    second_proj, first_part, cross = lax.psum((second_local, first_local, cross_local), "row")
    second_apply = jnp.dot(second_factor, second_proj, precision=highest).astype(jnp.bfloat16)
    first_proj = first_part - jnp.dot(cross, second_apply.astype(jnp.float32), precision=highest)
    first_apply = jnp.dot(first_factor, first_proj, precision=highest).astype(jnp.bfloat16)
    local_blocks = eigvecs.shape[0] // BLOCK
    columns = eigvecs.shape[1]
    width = reflectors.shape[2]
    local_index = region_blocks - lax.axis_index("row") * local_blocks
    picked_vecs = jnp.take(
        eigvecs.reshape(local_blocks, BLOCK, columns), local_index, axis=0
    ).reshape(-1, columns)
    picked_refl = jnp.take(
        reflectors.reshape(2, local_blocks, BLOCK, width), local_index, axis=1
    ).reshape(2, -1, width)
    region = picked_vecs.astype(jnp.float32)
    region = region - jnp.dot(picked_refl[1], second_apply, preferred_element_type=jnp.float32)
    region = region - jnp.dot(picked_refl[0], first_apply, preferred_element_type=jnp.float32)
    region = region.astype(jnp.bfloat16)
    weight_all = 1.0 / jnp.tanh(frequencies / 2.0) / (2.0 * frequencies)
    column_index = lax.axis_index("col")
    weight = lax.dynamic_slice_in_dim(weight_all, column_index * columns, columns, 0)
    scaled = (region.astype(jnp.float32) * weight[None, :]).astype(jnp.bfloat16)
    whole = lax.all_gather(region, "row", axis=0, tiled=True)
    partner = lax.all_to_all(whole, "col", split_axis=0, concat_axis=1, tiled=True)
    return contract_cols(lax.all_gather(scaled, "col", axis=1, tiled=True), partner)


def solution(mesh):
    return jax.shard_map(
        per_device,
        mesh=mesh,
        in_specs=(P("row", "col"), P(None, "row", None), P(), P(), P("row")),
        out_specs=P("row", "col"),
        check_vma=False,
    )
```

profile of v0, /device:TPU:6, one launch (start us, length us, event | category | flops | bytes accessed | tf_op | source)
XLA Modules:
  0.0 276.5 jit_solution(16794748032254373549)
XLA Ops:
  6.5 0.0 all-reduce.3.cloned.1.call-start
  6.5 0.0 copy-start
  6.5 0.0 slice-start
  6.5 4.2 %fusion.1 = f32[128,128]{1,0:T(8,128)} fusion(bf16[2,10240,128]{2,1,0:T(8,128)(2,1)} %param.6), kind=kOutput, calls=%fused_computation.5 | convolution fusion | flops 335544320 | bytes 5308416 | tf_op jit(solution)/shard_map/dot_general | solution.py:10
  10.7 0.0 copy-done
  10.7 0.0 slice-start.1
  10.7 3.7 %fusion.3 = f32[128,256]{1,0:T(8,128)} fusion(bf16[10240,256]{1,0:T(8,128)(2,1)S(1)} %copy-done, bf16[2,10240,128]{2,1,0:T(8,128)(2,1)} %param.6), kind=kOutput, calls=%fused_computation.7 | convolution fusion | flops 671088640 | bytes 7995392 | tf_op jit(solution)/shard_map/dot_general | solution.py:10
  14.4 0.0 slice-done
  14.4 0.0 slice-done.1
  14.4 0.0 copy-start.1
  14.4 1.7 fusion.6
  16.1 0.0 all-reduce.3.cloned.1.call-update
  16.1 0.0 all-gather.5.cloned.1.call-start
  16.2 0.0 copy-done.1
  16.2 0.1 broadcast_bitcast_fusion
  16.3 3.3 %gather_fusion.1 = bf16[18,2,128,128]{3,2,1,0:T(8,128)(2,1)S(1)} fusion(bf16[2,80,128,128]{3,2,1,0:T(8,128)(2,1)} %bitcast.43, s32[1024]{0:T(1024)S(1)} %pad_clamp_fusion), kind=kCustom, calls=%fused_computation.1 | custom fusion | bytes 2359368 | tf_op jit(solution)/shard_map/jit(_take)/gather | solution.py:41
  19.6 0.2 select_bitcast_fusion
  19.8 3.1 %gather_fusion = bf16[18,128,256]{2,1,0:T(8,128)(2,1)S(1)} fusion(bf16[80,128,256]{2,1,0:T(8,128)(2,1)} %bitcast.42, s32[1024]{0:T(1024)S(1)} %pad_clamp_fusion), kind=kCustom, calls=%fused_computation | custom fusion | bytes 2359368 | tf_op jit(solution)/shard_map/jit(_take)/gather | solution.py:38
  22.9 0.8 multiply_divide_fusion
  23.6 1.2 bitcast_select_fusion
  24.9 0.1 fusion.20
  25.0 29.0 %all-reduce.3.cloned.1.call-done = (f32[128,256]{1,0:T(8,128)}, f32[128,256]{1,0:T(8,128)}, f32[128,128]{1,0:T(8,128)}) async-done(((f32[128,256]{1,0:T(8,128)}, f32[128,256]{1,0:T(8,128)}, f32[128,128]{1,0:T(8,128)}), (f32[128,256]{1,0:T(8,128)}, f32[128,256]{1,0:T(8,128)}, f32[128,128]{1,0:T(8,128)})) %all-reduce.3.cloned.1.call-update) | async-done | bytes 327696 | tf_op jit(solution)/shard_map/psum | solution.py:30
  54.0 1.2 convolution_convert_fusion.1
  55.3 1.1 convolution_subtract_fusion.2
  56.4 1.1 convolution_convert_fusion
  57.6 0.5 convolution_subtract_fusion.1
  58.0 1.9 multiply_convert_fusion
  59.9 0.0 all-gather.5.cloned.1.call-update
  59.9 0.0 all-gather.3.cloned.1.call-start
  60.0 0.7 all-gather.3.cloned.1.call-update
  60.7 88.6 %all-gather.5.cloned.1.call-done = bf16[9216,256]{1,0:T(8,128)(2,1)} async-done(((bf16[2304,256]{1,0:T(8,128)(2,1)}), bf16[9216,256]{1,0:T(8,128)(2,1)}) %all-gather.5.cloned.1.call-update) | async-done | bytes 4718608 | tf_op jit(solution)/shard_map/all_gather | solution.py:52
  149.3 6.6 %copy.6 = bf16[8,1152,256]{1,2,0:T(8,128)(2,1)} copy(bf16[8,1152,256]{2,1,0:T(8,128)(2,1)} %bitcast.46) | data formatting | bytes 9437184 | tf_op jit(solution)/shard_map/all_to_all | solution.py:53
  155.9 83.3 %all_to_all.19 = bf16[8,1152,256]{1,2,0:T(8,128)(2,1)} all-to-all(bf16[8,1152,256]{1,2,0:T(8,128)(2,1)} %copy.6), channel_id=1, replica_groups=mesh['row'=4,'col'=8] {'col'}, dimensions={0} | all-to-all | bytes 9437184 | tf_op jit(solution)/shard_map/all_to_all | solution.py:53
  239.2 13.0 %all-gather.3.cloned.1.call-done = bf16[2304,2048]{1,0:T(8,128)(2,1)} async-done(((bf16[2304,256]{1,0:T(8,128)(2,1)}), bf16[2304,2048]{1,0:T(8,128)(2,1)}) %all-gather.3.cloned.1.call-update) | async-done | bytes 9437200 | tf_op jit(solution)/shard_map/all_gather | solution.py:54
  252.2 17.8 %fusion.21 = f32[2304,1152]{1,0:T(8,128)} fusion(bf16[2304,2048]{1,0:T(8,128)(2,1)} %all-gather.3.cloned.1.call-done, bf16[1152,2048]{0,1:T(8,128)(2,1)} %bitcast.47), kind=kOutput, calls=%fused_computation.40 | convolution fusion | flops 10871635968 | bytes 24772608 | tf_op jit(solution)/shard_map/dot_general | solution.py:16
  (4 shorter events, 0.0 us)
Async XLA Ops:
  6.5 47.5 %all-reduce.3.cloned.1.call-start = ((), (), s32[]{:S(2)}) async-start(), calls=%async_computation.3 | async-start | bytes 655360 | tf_op jit(solution)/shard_map/psum | solution.py:30
  6.5 4.2 %copy-start = (bf16[10240,256]{1,0:T(8,128)(2,1)S(1)}, bf16[10240,256]{1,0:T(8,128)(2,1)}, u32[]{:S(2)}) copy-start(bf16[10240,256]{1,0:T(8,128)(2,1)} %param.5) | copy-start | bytes 15728644
  6.5 7.9 %slice-start = ((s8[5242880]{0:T(1024)(128)(4,1)}), s8[4194304]{0:T(1024)(128)(4,1)S(1)}, s32[]{:S(2)}) async-start(s8[5242880]{0:T(1024)(128)(4,1)} %bitcast.44), calls=%async_computation.4 | async-start | bytes 8388608
  10.7 3.7 %slice-start.1 = ((s8[5242880]{0:T(1024)(128)(4,1)}), s8[1048576]{0:T(1024)(128)(4,1)S(1)}, s32[]{:S(2)}) async-start(s8[5242880]{0:T(1024)(128)(4,1)} %bitcast.44), calls=%async_computation.5 | async-start | bytes 2097152
  14.4 1.8 copy-start.1
  16.1 133.1 %all-gather.5.cloned.1.call-start = ((), (), s32[]{:S(2)}) async-start(), calls=%async_computation.2 | async-start | bytes 5898240 | tf_op jit(solution)/shard_map/all_gather | solution.py:52
  59.9 192.3 %all-gather.3.cloned.1.call-start = ((), (), s32[]{:S(2)}) async-start(), calls=%async_computation.1 | async-start | bytes 10616832 | tf_op jit(solution)/shard_map/all_gather | solution.py:54
Sparse Core Ops, SparseCore 0:
  16.3 37.7 all-reduce.2
  60.0 89.1 all-gather.4
  151.1 101.0 all-gather.2
where the time goes:
time: 279 us; the launch traced here: 277 us
  waiting for transfers between devices  131 us (47%)
  blocking collectives  83.3 us (30%)
  matrix products  33.2 us (12%)
  local copies, waits for them, and re-layouts  13.2 us (5%)
  between operations  13.2 us (5%)
    all_gather x1, waiting for transfers between devices, per_device(): whole = lax.all_gather(region, 'row', axis=0, tiled=True)  88.6 us
    all_to_all x1, blocking collectives, per_device(): lax.all_to_all(whole, 'col', split_axis=0, concat_axis=1, tiled=True)  83.3 us
    psum x1, waiting for transfers between devices, per_device(): lax.psum((second_local, first_local, cross_local), 'row')  29 us
    dot_general x1, matrix products, contract_cols(): lax.dot_general(left, right, (((1,), (1,)), ((), ())), preferred_element_...  17.8 us
    all_gather x1, waiting for transfers between devices, per_device(): lax.all_gather(scaled, 'col', axis=1, tiled=True)  13 us
    dot_general x3, matrix products, contract_rows(): lax.dot_general(left, right, (((0,), (0,)), ((), ())), preferred_element_...  9.56 us
    all_to_all x1, local copies, waits for them, and re-layouts, per_device(): lax.all_to_all(whole, 'col', split_axis=0, concat_axis=1, tiled=True)  6.62 us
  transfers between devices with their start and end apart: 3, of which 3 were waited for; matrix products, arithmetic and copies ran while one was open for 6% of the time, Pallas kernels for 0%

commit v1 on v0

--- a/solution.py
+++ b/solution.py
@@ -1,9 +1,15 @@
+import functools
+
 import jax
 import jax.numpy as jnp
 from jax import lax
+from jax.experimental import pallas as pl
+from jax.experimental.pallas import tpu as pltpu
 from jax.sharding import PartitionSpec as P
 
 BLOCK = 128
+MESH = pl.DeviceIdType.MESH
+SUB = 8
 
 
 def contract_rows(left, right):
@@ -18,7 +24,206 @@
     )
 
 
-def per_device(eigvecs, reflectors, factors, frequencies, region_blocks):
+def exchange_kernel(
+    n_row, sub, x_ref, a_ref, b_ref, half_buf,
+    own_sem, send_plane, send_sib, recv_a, send_z, recv_b, fill_sem,
+):
+    r = lax.axis_index("row")
+    c = lax.axis_index("col")
+    k = c // 2
+    h = lax.rem(c, 2)
+    o = 1 - h
+    sib = 2 * k + o
+    rows, cols = x_ref.shape
+    step = rows // sub
+    hsub = sub // 2
+    half = rows // 2
+    has_up = (r < n_row - 1).astype(jnp.int32)
+    has_dn = (r > 0).astype(jnp.int32)
+
+    barrier = pltpu.get_barrier_semaphore()
+
+    def greet(row, col):
+        pl.semaphore_signal(barrier, inc=1, device_id=(row, col), device_id_type=MESH)
+
+    greet(r, sib)
+    for d in range(1, n_row):
+        greet(r, 2 * (k ^ d) + h)
+
+    @pl.when(r < n_row - 1)
+    def _():
+        greet(r + 1, c)
+
+    @pl.when(r > 0)
+    def _():
+        greet(r - 1, c)
+
+    pl.semaphore_wait(barrier, n_row + has_up + has_dn)
+
+    def piece_cols(d, side):
+        owner = 2 * (k ^ d) + (h if side == 0 else o)
+        return pl.ds(pl.multiple_of(owner * cols, cols), cols)
+
+    def a_at(d, side, s):
+        return a_ref.at[pl.ds(s * step, step), piece_cols(d, side)]
+
+    def plane_copy(d, s):
+        return pltpu.make_async_remote_copy(
+            src_ref=x_ref.at[pl.ds(s * step, step), :],
+            dst_ref=a_ref.at[pl.ds(s * step, step), piece_cols(0, 0)],
+            send_sem=send_plane.at[d, s], recv_sem=recv_a.at[d, 0, s],
+            device_id=(r, 2 * (k ^ d) + h), device_id_type=MESH,
+        )
+
+    def sib_copy(d, s):
+        src = x_ref.at[pl.ds(s * step, step), :] if d == 0 else a_at(d, 0, s)
+        return pltpu.make_async_remote_copy(
+            src_ref=src, dst_ref=a_at(d, 0, s),
+            send_sem=send_sib.at[d, s], recv_sem=recv_a.at[d, 1, s],
+            device_id=(r, sib), device_id_type=MESH,
+        )
+
+    def half_rows(t):
+        return pl.ds(pl.multiple_of(h * half + t * step, step), step)
+
+    def z_copy(src, way, target, d, side, t):
+        return pltpu.make_async_remote_copy(
+            src_ref=src,
+            dst_ref=b_ref.at[pl.ds(t * step, step), piece_cols(d, side)],
+            send_sem=send_z.at[way, d, side, t], recv_sem=recv_b.at[d, side, t],
+            device_id=(target, c), device_id_type=MESH,
+        )
+
+    def from_source(way, target, d, side, t):
+        if d == 0 and side == 0:
+            src = x_ref.at[half_rows(t), :]
+        else:
+            src = a_ref.at[half_rows(t), piece_cols(d, side)]
+        return z_copy(src, way, target, d, side, t)
+
+    def relay(way, target, d, side, t):
+        src = b_ref.at[pl.ds(t * step, step), piece_cols(d, side)]
+        return z_copy(src, way, target, d, side, t)
+
+    own = pltpu.make_async_copy(x_ref, a_ref.at[:, piece_cols(0, 0)], own_sem)
+    own.start()
+    for s in range(sub):
+        sib_copy(0, s).start()
+    for d in range(1, n_row):
+        for s in range(sub):
+            plane_copy(d, s).start()
+
+    arrivals = [(d, s) for d in range(1, n_row) for s in range(sub)]
+    parts = [(d, side, t) for d in range(n_row) for side in (0, 1) for t in range(hsub)]
+
+    def take_a(d, s):
+        plane_copy(d, s).wait_recv()
+        sib_copy(d, s).start()
+
+    at_source = r == k
+    above = r > k
+    below = r < k
+
+    @pl.when(at_source)
+    def _():
+        def push(d, side, t):
+            @pl.when(r < n_row - 1)
+            def _():
+                from_source(0, r + 1, d, side, t).start()
+
+            @pl.when(r > 0)
+            def _():
+                from_source(1, r - 1, d, side, t).start()
+
+        for d in range(n_row):
+            if d:
+                for s in range(sub):
+                    take_a(d, s)
+            else:
+                for t in range(hsub):
+                    push(d, 0, t)
+            for s in range(sub):
+                sib_copy(d, s).wait_recv()
+            for side in (0, 1) if d else (1,):
+                for t in range(hsub):
+                    push(d, side, t)
+        own.wait()
+        fill = pltpu.make_async_copy(
+            a_ref.at[pl.ds(pl.multiple_of(h * half, half), half), :], half_buf, fill_sem
+        )
+        fill.start()
+        fill.wait()
+        out = pltpu.make_async_copy(half_buf, b_ref, fill_sem)
+        out.start()
+        out.wait()
+
+    @pl.when(jnp.logical_not(at_source))
+    def _():
+        for i, (d, side, t) in enumerate(parts):
+            if i < len(arrivals):
+                take_a(*arrivals[i])
+            relay(0, r, d, side, t).wait_recv()
+
+            @pl.when(above & (r < n_row - 1))
+            def _():
+                relay(0, r + 1, d, side, t).start()
+
+            @pl.when(below & (r > 0))
+            def _():
+                relay(1, r - 1, d, side, t).start()
+
+        for d, s in arrivals[len(parts):]:
+            take_a(d, s)
+        for d in range(n_row):
+            for s in range(sub):
+                sib_copy(d, s).wait_recv()
+        own.wait()
+
+    for d in range(n_row):
+        for s in range(sub):
+            sib_copy(d, s).wait_send()
+            if d:
+                plane_copy(d, s).wait_send()
+    for d, side, t in parts:
+        @pl.when((r >= k) & (r < n_row - 1))
+        def _():
+            relay(0, r, d, side, t).wait_send()
+
+        @pl.when((r <= k) & (r > 0))
+        def _():
+            relay(1, r, d, side, t).wait_send()
+
+
+def exchange(x, n_row):
+    rows, cols = x.shape
+    n_col = 2 * n_row
+    sub = SUB if n_row <= 4 else SUB // 2
+    hsub = sub // 2
+    dma = pltpu.SemaphoreType.DMA
+    return pl.pallas_call(
+        functools.partial(exchange_kernel, n_row, sub),
+        out_shape=(
+            jax.ShapeDtypeStruct((rows, cols * n_col), x.dtype),
+            jax.ShapeDtypeStruct((rows // 2, cols * n_col), x.dtype),
+        ),
+        in_specs=[pl.BlockSpec(memory_space=pltpu.VMEM)],
+        out_specs=(pl.BlockSpec(memory_space=pl.ANY),) * 2,
+        scratch_shapes=[
+            pltpu.VMEM((rows // 2, cols * n_col), x.dtype),
+            dma,
+            dma((n_row, sub)),
+            dma((n_row, sub)),
+            dma((n_row, 2, sub)),
+            dma((2, n_row, 2, hsub)),
+            dma((n_row, 2, hsub)),
+            dma,
+        ],
+        compiler_params=pltpu.CompilerParams(collective_id=0, has_side_effects=True),
+        name="exchange",
+    )(x)
+
+
+def per_device(n_row, eigvecs, reflectors, factors, frequencies, region_blocks):
     highest = lax.Precision.HIGHEST
     first_block = reflectors[0]
     second_block = reflectors[1]
@@ -45,18 +250,15 @@
     region = region - jnp.dot(picked_refl[1], second_apply, preferred_element_type=jnp.float32)
     region = region - jnp.dot(picked_refl[0], first_apply, preferred_element_type=jnp.float32)
     region = region.astype(jnp.bfloat16)
-    weight_all = 1.0 / jnp.tanh(frequencies / 2.0) / (2.0 * frequencies)
-    column_index = lax.axis_index("col")
-    weight = lax.dynamic_slice_in_dim(weight_all, column_index * columns, columns, 0)
-    scaled = (region.astype(jnp.float32) * weight[None, :]).astype(jnp.bfloat16)
-    whole = lax.all_gather(region, "row", axis=0, tiled=True)
-    partner = lax.all_to_all(whole, "col", split_axis=0, concat_axis=1, tiled=True)
-    return contract_cols(lax.all_gather(scaled, "col", axis=1, tiled=True), partner)
+    weight = 1.0 / jnp.tanh(frequencies / 2.0) / (2.0 * frequencies)
+    mine, partner = exchange(region, n_row)
+    scaled = (mine.astype(jnp.float32) * weight[None, :]).astype(jnp.bfloat16)
+    return contract_cols(scaled, partner)
 
 
 def solution(mesh):
     return jax.shard_map(
-        per_device,
+        functools.partial(per_device, mesh.shape["row"]),
         mesh=mesh,
         in_specs=(P("row", "col"), P(None, "row", None), P(), P(), P("row")),
         out_specs=P("row", "col"),

time: 279 us -> 206 us (0.74)
  Pallas kernels: 0 us -> 122 us
  waiting for transfers between devices: 131 us -> 29.8 us
  blocking collectives: 83.3 us -> 0 us
  local copies, waits for them, and re-layouts: 13.2 us -> 6.58 us
    pallas_call x0 -> x1, Pallas kernels: none -> 122 us  [exchange(): pl.pallas_call(functools.partial(exchange_kernel, n_row, sub), out_shape=...]
    all_gather x2 -> x0, waiting for transfers between devices: 102 us -> none  [the longest x1 88.6 us: per_device(): whole = lax.all_gather(region, 'row', axis=0, tiled=True)]
    all_to_all x1 -> x0, blocking collectives: 83.3 us -> none  [per_device(): lax.all_to_all(whole, 'col', split_axis=0, concat_axis=1, tiled=True)]
    all_to_all x1 -> x0, local copies, waits for them, and re-layouts: 6.62 us -> none  [per_device(): lax.all_to_all(whole, 'col', split_axis=0, concat_axis=1, tiled=True)]
  transfers between devices with their start and end apart: 3 -> 1, of which waited for: 3 -> 1; matrix products, arithmetic and copies ran while one was open for 6% -> 4% of each run, Pallas kernels for 0% -> 0%
where the time goes in v1:
time: 206 us
  Pallas kernels  122 us (59%)
  matrix products  32.9 us (16%)
  waiting for transfers between devices  29.8 us (14%)
  between operations  13.5 us (7%)
  local copies, waits for them, and re-layouts  6.58 us (3%)
    pallas_call x1, Pallas kernels, exchange(): pl.pallas_call(functools.partial(exchange_kernel, n_row, sub), out_shape=...  122 us
    psum x1, waiting for transfers between devices, per_device(): lax.psum((second_local, first_local, cross_local), 'row')  29.8 us
    dot_general x1, matrix products, contract_cols(): lax.dot_general(left, right, (((1,), (1,)), ((), ())), preferred_element_...  17.9 us
    dot_general x3, matrix products, contract_rows(): lax.dot_general(left, right, (((0,), (0,)), ((), ())), preferred_element_...  9.57 us
  transfers between devices with their start and end apart: 1, of which 1 were waited for; matrix products, arithmetic and copies ran while one was open for 4% of the time, Pallas kernels for 0%

profile of v1, /device:TPU:6, one launch (start us, length us, event | category | flops | bytes accessed | tf_op | source)
XLA Modules:
  0.0 206.0 jit_solution(3189538724953506353)
XLA Ops:
  6.5 0.0 all-reduce.3.cloned.1.call-start
  6.5 0.0 copy-start
  6.5 0.0 slice-start
  6.5 4.2 %fusion.3 = f32[128,128]{1,0:T(8,128)} fusion(bf16[2,10240,128]{2,1,0:T(8,128)(2,1)} %param.6), kind=kOutput, calls=%fused_computation.8 | convolution fusion | flops 335544320 | bytes 5308416 | tf_op jit(solution)/shard_map/dot_general | solution.py:16
  10.7 0.0 copy-done
  10.7 0.0 slice-start.1
  10.7 3.7 %fusion.5 = f32[128,256]{1,0:T(8,128)} fusion(bf16[10240,256]{1,0:T(8,128)(2,1)S(1)} %copy-done, bf16[2,10240,128]{2,1,0:T(8,128)(2,1)} %param.6), kind=kOutput, calls=%fused_computation.10 | convolution fusion | flops 671088640 | bytes 7995392 | tf_op jit(solution)/shard_map/dot_general | solution.py:16
  14.4 0.0 slice-done
  14.4 0.0 slice-done.1
  14.4 0.0 copy-start.2
  14.4 0.0 copy-start.1
  14.5 1.7 fusion.8
  16.1 0.0 all-reduce.3.cloned.1.call-update
  16.2 0.0 copy-done.2
  16.2 0.1 broadcast_bitcast_fusion
  16.3 0.0 copy-done.1
  16.3 3.3 %gather_fusion.1 = bf16[18,2,128,128]{3,2,1,0:T(8,128)(2,1)S(1)} fusion(bf16[2,80,128,128]{3,2,1,0:T(8,128)(2,1)} %bitcast.38, s32[1024]{0:T(1024)S(1)} %pad_clamp_fusion), kind=kCustom, calls=%fused_computation.1 | custom fusion | bytes 2359368 | tf_op jit(solution)/shard_map/jit(_take)/gather | solution.py:246
  19.6 0.2 select_bitcast_fusion
  19.8 3.1 %gather_fusion = bf16[18,128,256]{2,1,0:T(8,128)(2,1)S(1)} fusion(bf16[80,128,256]{2,1,0:T(8,128)(2,1)} %bitcast.37, s32[1024]{0:T(1024)S(1)} %pad_clamp_fusion), kind=kCustom, calls=%fused_computation | custom fusion | bytes 2359368 | tf_op jit(solution)/shard_map/jit(_take)/gather | solution.py:243
  22.9 1.2 bitcast_select_fusion
  24.1 0.1 fusion.22
  24.3 29.8 %all-reduce.3.cloned.1.call-done = (f32[128,256]{1,0:T(8,128)}, f32[128,256]{1,0:T(8,128)}, f32[128,128]{1,0:T(8,128)}) async-done(((f32[128,256]{1,0:T(8,128)}, f32[128,256]{1,0:T(8,128)}, f32[128,128]{1,0:T(8,128)}), (f32[128,256]{1,0:T(8,128)}, f32[128,256]{1,0:T(8,128)}, f32[128,128]{1,0:T(8,128)})) %all-reduce.3.cloned.1.call-update) | async-done | bytes 327696 | tf_op jit(solution)/shard_map/psum | solution.py:235
  54.0 1.2 convolution_convert_fusion.1
  55.3 1.1 convolution_subtract_fusion.2
  56.4 1.1 convolution_convert_fusion
  57.6 0.5 convolution_subtract_fusion.1
  58.0 1.5 fusion.2.x_ref
  59.5 121.8 %exchange.1 = (bf16[2304,2048]{1,0:T(8,128)(2,1)}, bf16[1152,2048]{1,0:T(8,128)(2,1)}) custom-call(bf16[2304,256]{1,0:T(8,128)(2,1)} %fusion.2.x_ref), custom_call_target="tpu_custom_call" | custom-call | tf_op jit(solution)/shard_map/exchange/pallas_call | solution.py:203
  181.3 17.9 %fusion = f32[2304,1152]{1,0:T(8,128)} fusion(bf16[1152,2048]{1,0:T(8,128)(2,1)} %get-tuple-element.8, bf16[2304,2048]{1,0:T(8,128)(2,1)} %get-tuple-element.7, f32[2048]{0:T(1024)S(1)} %multiply_divide_fusion), kind=kOutput, calls=%fused_computation.3 | convolution fusion | flops 10885791744 | bytes 24780800 | tf_op jit(solution)/shard_map/dot_general | solution.py:22
  (5 shorter events, 0.0 us)
Async XLA Ops:
  6.5 47.5 %all-reduce.3.cloned.1.call-start = ((), (), s32[]{:S(2)}) async-start(), calls=%async_computation | async-start | bytes 655360 | tf_op jit(solution)/shard_map/psum | solution.py:235
  6.5 4.2 %copy-start = (bf16[10240,256]{1,0:T(8,128)(2,1)S(1)}, bf16[10240,256]{1,0:T(8,128)(2,1)}, u32[]{:S(2)}) copy-start(bf16[10240,256]{1,0:T(8,128)(2,1)} %param.5) | copy-start | bytes 15728644
  6.5 7.9 %slice-start = ((s8[5242880]{0:T(1024)(128)(4,1)}), s8[4194304]{0:T(1024)(128)(4,1)S(1)}, s32[]{:S(2)}) async-start(s8[5242880]{0:T(1024)(128)(4,1)} %bitcast.39), calls=%async_computation.1 | async-start | bytes 8388608
  10.7 3.7 %slice-start.1 = ((s8[5242880]{0:T(1024)(128)(4,1)}), s8[1048576]{0:T(1024)(128)(4,1)S(1)}, s32[]{:S(2)}) async-start(s8[5242880]{0:T(1024)(128)(4,1)} %bitcast.39), calls=%async_computation.2 | async-start | bytes 2097152
  14.4 1.7 copy-start.2
  14.4 1.8 copy-start.1
Sparse Core Ops, SparseCore 0:
  16.3 37.6 all-reduce.2

commit v2 on v1

--- a/solution.py
+++ b/solution.py
@@ -223,33 +223,157 @@
     )(x)
 
 
+def project_kernel(
+    n_row, w_ref, g_ref, t_ref, p_ref,
+    w_in, g_in, w_sum, g_sum, w_full, g_full, send_1, recv_1, send_2, recv_2,
+):
+    r = lax.axis_index("row")
+    c = lax.axis_index("col")
+    barrier = pltpu.get_barrier_semaphore()
+    for d in range(1, n_row):
+        pl.semaphore_signal(barrier, inc=1, device_id=(r ^ d, c), device_id_type=MESH)
+    pl.semaphore_wait(barrier, n_row - 1)
+    pairs = ((w_ref, w_in, w_sum, w_full), (g_ref, g_in, g_sum, g_full))
+
+    def part(array, owner):
+        size = array.shape[0] // n_row
+        return pl.ds(pl.multiple_of(owner * size, size), size)
+
+    def scatter(d, i):
+        array, landing, _, _ = pairs[i]
+        return pltpu.make_async_remote_copy(
+            src_ref=array.at[part(array, r ^ d), :], dst_ref=landing.at[d],
+            send_sem=send_1.at[d, i], recv_sem=recv_1.at[d, i],
+            device_id=(r ^ d, c), device_id_type=MESH,
+        )
+
+    def spread(d, i):
+        array, _, total, full = pairs[i]
+        return pltpu.make_async_remote_copy(
+            src_ref=total, dst_ref=full.at[part(array, r), :],
+            send_sem=send_2.at[d, i], recv_sem=recv_2.at[d, i],
+            device_id=(r ^ d, c), device_id_type=MESH,
+        )
+
+    every = [(d, i) for d in range(1, n_row) for i in (1, 0)]
+    for d, i in every:
+        scatter(d, i).start()
+    for d, i in every:
+        scatter(d, i).wait_recv()
+    for i in (1, 0):
+        array, landing, total, full = pairs[i]
+        value = array[part(array, r), :]
+        for d in range(1, n_row):
+            value = value + landing[d]
+        total[...] = value
+    for i in (1, 0):
+        array, _, total, full = pairs[i]
+        full[part(array, r), :] = total[...]
+    for d, i in every:
+        spread(d, i).start()
+    for d, i in every:
+        spread(d, i).wait_recv()
+    highest = lax.Precision.HIGHEST
+    width = g_ref.shape[0]
+    second = jnp.dot(
+        t_ref[1], w_full[width:, :], precision=highest, preferred_element_type=jnp.float32
+    ).astype(jnp.bfloat16)
+    first = w_full[:width, :] - jnp.dot(
+        g_full[...], second.astype(jnp.float32),
+        precision=highest, preferred_element_type=jnp.float32,
+    )
+    first = jnp.dot(t_ref[0], first, precision=highest, preferred_element_type=jnp.float32)
+    p_ref[0] = first.astype(jnp.bfloat16)
+    p_ref[1] = second
+    for d, i in every:
+        scatter(d, i).wait_send()
+        spread(d, i).wait_send()
+
+
+def project(w, g, factors, n_row):
+    dma = pltpu.SemaphoreType.DMA((n_row, 2))
+    width, columns = g.shape[0], w.shape[1]
+    vmem = pl.BlockSpec(memory_space=pltpu.VMEM)
+
+    def landing(array):
+        return pltpu.VMEM((n_row, array.shape[0] // n_row, array.shape[1]), jnp.float32)
+
+    def total(array):
+        return pltpu.VMEM((array.shape[0] // n_row, array.shape[1]), jnp.float32)
+
+    return pl.pallas_call(
+        functools.partial(project_kernel, n_row),
+        out_shape=jax.ShapeDtypeStruct((2, width, columns), jnp.bfloat16),
+        in_specs=[vmem] * 3,
+        out_specs=vmem,
+        scratch_shapes=[
+            landing(w), landing(g), total(w), total(g),
+            pltpu.VMEM(w.shape, jnp.float32), pltpu.VMEM(g.shape, jnp.float32),
+            dma, dma, dma, dma,
+        ],
+        compiler_params=pltpu.CompilerParams(collective_id=1, has_side_effects=True),
+        name="project",
+    )(w, g, factors)
+
+
+def region_kernel(index_ref, p_ref, vecs_ref, refl_ref, out_ref, vecs, refl, sems):
+    count = vecs.shape[0]
+
+    def copies(b):
+        at = index_ref[b]
+        return (
+            pltpu.make_async_copy(vecs_ref.at[at], vecs.at[b], sems.at[b, 0]),
+            pltpu.make_async_copy(refl_ref.at[0, at], refl.at[0, b], sems.at[b, 1]),
+            pltpu.make_async_copy(refl_ref.at[1, at], refl.at[1, b], sems.at[b, 2]),
+        )
+
+    for b in range(count):
+        for copy in copies(b):
+            copy.start()
+    for b in range(count):
+        for copy in copies(b):
+            copy.wait()
+        value = vecs[b].astype(jnp.float32)
+        value = value - jnp.dot(refl[1, b], p_ref[1], preferred_element_type=jnp.float32)
+        value = value - jnp.dot(refl[0, b], p_ref[0], preferred_element_type=jnp.float32)
+        out_ref[b] = value.astype(out_ref.dtype)
+
+
+def region_rows(index, applied, vecs, refl):
+    count = index.shape[0]
+    columns, width = vecs.shape[2], refl.shape[3]
+    vmem = pl.BlockSpec(memory_space=pltpu.VMEM)
+    hbm = pl.BlockSpec(memory_space=pl.ANY)
+    return pl.pallas_call(
+        region_kernel,
+        out_shape=jax.ShapeDtypeStruct((count, BLOCK, columns), vecs.dtype),
+        in_specs=[pl.BlockSpec(memory_space=pltpu.SMEM), vmem, hbm, hbm],
+        out_specs=vmem,
+        scratch_shapes=[
+            pltpu.VMEM((count, BLOCK, columns), vecs.dtype),
+            pltpu.VMEM((2, count, BLOCK, width), refl.dtype),
+            pltpu.SemaphoreType.DMA((count, 3)),
+        ],
+        name="region",
+    )(index, applied, vecs, refl)
+
+
 def per_device(n_row, eigvecs, reflectors, factors, frequencies, region_blocks):
-    highest = lax.Precision.HIGHEST
-    first_block = reflectors[0]
-    second_block = reflectors[1]
-    first_factor = jnp.triu(factors[0])
-    second_factor = jnp.triu(factors[1])
-    second_local = contract_rows(second_block, eigvecs)
-    first_local = contract_rows(first_block, eigvecs)
-    cross_local = contract_rows(first_block, second_block)
-    second_proj, first_part, cross = lax.psum((second_local, first_local, cross_local), "row")
-    second_apply = jnp.dot(second_factor, second_proj, precision=highest).astype(jnp.bfloat16)
-    first_proj = first_part - jnp.dot(cross, second_apply.astype(jnp.float32), precision=highest)
-    first_apply = jnp.dot(first_factor, first_proj, precision=highest).astype(jnp.bfloat16)
-    local_blocks = eigvecs.shape[0] // BLOCK
     columns = eigvecs.shape[1]
     width = reflectors.shape[2]
+    local = lax.dot_general(
+        reflectors, eigvecs, (((1,), (0,)), ((), ())), preferred_element_type=jnp.float32
+    ).reshape(2 * width, columns)
+    cross_local = contract_rows(reflectors[0], reflectors[1])
+    applied = project(local, cross_local, jnp.triu(factors), n_row)
+    local_blocks = eigvecs.shape[0] // BLOCK
     local_index = region_blocks - lax.axis_index("row") * local_blocks
-    picked_vecs = jnp.take(
-        eigvecs.reshape(local_blocks, BLOCK, columns), local_index, axis=0
+    region = region_rows(
+        local_index,
+        applied,
+        eigvecs.reshape(local_blocks, BLOCK, columns),
+        reflectors.reshape(2, local_blocks, BLOCK, width),
     ).reshape(-1, columns)
-    picked_refl = jnp.take(
-        reflectors.reshape(2, local_blocks, BLOCK, width), local_index, axis=1
-    ).reshape(2, -1, width)
-    region = picked_vecs.astype(jnp.float32)
-    region = region - jnp.dot(picked_refl[1], second_apply, preferred_element_type=jnp.float32)
-    region = region - jnp.dot(picked_refl[0], first_apply, preferred_element_type=jnp.float32)
-    region = region.astype(jnp.bfloat16)
     weight = 1.0 / jnp.tanh(frequencies / 2.0) / (2.0 * frequencies)
     mine, partner = exchange(region, n_row)
     scaled = (mine.astype(jnp.float32) * weight[None, :]).astype(jnp.bfloat16)

time: 206 us -> 179 us (0.87)
  waiting for transfers between devices: 29.8 us -> 0 us
  Pallas kernels: 122 us -> 149 us
  between operations: 13.5 us -> 0.04 us
  local copies, waits for them, and re-layouts: 6.58 us -> 0.01 us
  matrix products: 32.9 us -> 26.7 us
    psum x1 -> x0, waiting for transfers between devices: 29.8 us -> none  [per_device(): lax.psum((second_local, first_local, cross_local), 'row')]
    pallas_call x0 -> x2, Pallas kernels: none -> 27.3 us  [the longest x1 20.8 us: project(): pl.pallas_call(functools.partial(project_kernel, n_row), out_shape=jax.Sh...]
    gather x2 -> x0, local copies, waits for them, and re-layouts: 6.37 us -> none  [the longest x1 3.26 us: per_device(): jnp.take(reflectors.reshape(2, local_blocks, BLOCK, width), local_index,...]
    dot_general x3 -> x1, matrix products: 9.57 us -> 4.06 us  [contract_rows(): lax.dot_general(left, right, (((0,), (0,)), ((), ())), preferred_element_...]
    dot_general x5 -> x1, matrix products: 5.47 us -> 4.79 us  [per_device(): lax.dot_general(reflectors, eigvecs, (((1,), (0,)), ((), ())), preferred_...]
  transfers between devices with their start and end apart: 1 -> 0, of which waited for: 1 -> 0; matrix products, arithmetic and copies ran while one was open for 4% -> 0% of each run, Pallas kernels for 0% -> 0%
where the time goes in v2:
time: 179 us
  Pallas kernels  149 us (83%)
  matrix products  26.7 us (15%)
  other arithmetic  3.08 us (2%)
    pallas_call x1, Pallas kernels, exchange(): pl.pallas_call(functools.partial(exchange_kernel, n_row, sub), out_shape=...  122 us
    pallas_call x1, Pallas kernels, project(): pl.pallas_call(functools.partial(project_kernel, n_row), out_shape=jax.Sh...  20.8 us
    dot_general x1, matrix products, contract_cols(): lax.dot_general(left, right, (((1,), (1,)), ((), ())), preferred_element_...  17.9 us
    pallas_call x1, Pallas kernels, region_rows(): pl.pallas_call(region_kernel, out_shape=jax.ShapeDtypeStruct((count, BLOC...  6.48 us
    dot_general x1, matrix products, per_device(): lax.dot_general(reflectors, eigvecs, (((1,), (0,)), ((), ())), preferred_...  4.79 us
    dot_general x1, matrix products, contract_rows(): lax.dot_general(left, right, (((0,), (0,)), ((), ())), preferred_element_...  4.06 us

profile of v2, /device:TPU:6, one launch (start us, length us, event | category | flops | bytes accessed | tf_op | source)
XLA Modules:
  0.0 178.9 jit_solution(14373097069038042372)
XLA Ops:
  0.0 0.0 copy-start.1
  0.0 0.0 copy-start
  0.0 1.4 broadcast_subtract_fusion.index_ref
  1.4 1.0 multiply_divide_fusion
  2.3 0.1 iota_compare_fusion
  2.4 4.1 %fusion.4.g_ref = f32[128,128]{1,0:T(8,128)} fusion(bf16[2,10240,128]{2,1,0:T(8,128)(2,1)} %param.6), kind=kOutput, calls=%fused_computation.5 | convolution fusion | flops 335544320 | bytes 5308416 | tf_op jit(solution)/shard_map/dot_general | solution.py:16
  6.5 0.0 copy-done.1
  6.5 0.7 broadcast_select_fusion.t_ref
  7.1 0.0 copy-done
  7.2 4.8 %fusion.2 = f32[2,128,256]{2,1,0:T(8,128)} fusion(bf16[2,10240,128]{2,1,0:T(8,128)(2,1)S(1)} %copy-done, bf16[10240,256]{1,0:T(8,128)(2,1)} %param.5), kind=kOutput, calls=%fused_computation.3 | convolution fusion | flops 1342177280 | bytes 10747904 | tf_op jit(solution)/shard_map/dot_general | solution.py:364
  11.9 20.8 %project.1.p_ref = bf16[2,128,256]{2,1,0:T(8,128)(2,1)} custom-call(f32[256,256]{1,0:T(8,128)} %bitcast.18, f32[128,128]{1,0:T(8,128)} %fusion.4.g_ref, f32[2,128,128]{2,1,0:T(8,128)} %broadcast_select_fusion.t_ref), custom_call_target="tpu_custom_call" | custom-call | tf_op jit(solution)/shard_map/project/pallas_call | solution.py:304
  32.8 6.5 %region.1 = bf16[18,128,256]{2,1,0:T(8,128)(2,1)} custom-call(s32[18]{0:T(128)} %broadcast_subtract_fusion.index_ref, bf16[2,128,256]{2,1,0:T(8,128)(2,1)} %project.1.p_ref, bf16[80,128,256]{2,1,0:T(8,128)(2,1)} %bitcast.16, bf16[2,80,128,128]{3,2,1,0:T(8,128)(2,1)} %bitcast.15), custom_call_target="tpu_custom_call" | custom-call | tf_op jit(solution)/shard_map/region/pallas_call | solution.py:347
  39.2 121.8 %exchange.1 = (bf16[2304,2048]{1,0:T(8,128)(2,1)}, bf16[1152,2048]{1,0:T(8,128)(2,1)}) custom-call(bf16[2304,256]{1,0:T(8,128)(2,1)} %bitcast.17), custom_call_target="tpu_custom_call" | custom-call | tf_op jit(solution)/shard_map/exchange/pallas_call | solution.py:203
  161.0 17.9 %fusion = f32[2304,1152]{1,0:T(8,128)} fusion(bf16[1152,2048]{1,0:T(8,128)(2,1)} %get-tuple-element.8, bf16[2304,2048]{1,0:T(8,128)(2,1)} %get-tuple-element.7, f32[2048]{0:T(1024)S(1)} %multiply_divide_fusion), kind=kOutput, calls=%fused_computation.1 | convolution fusion | flops 10885791744 | bytes 24780800 | tf_op jit(solution)/shard_map/dot_general | solution.py:22
  (1 shorter events, 0.0 us)
Async XLA Ops:
  0.0 6.5 %copy-start.1 = (f32[2,128,128]{2,1,0:T(8,128)S(1)}, f32[2,128,128]{2,1,0:T(8,128)}, u32[]{:S(2)}) copy-start(f32[2,128,128]{2,1,0:T(8,128)} %param.7) | copy-start | bytes 393220
  0.0 7.1 %copy-start = (bf16[2,10240,128]{2,1,0:T(8,128)(2,1)S(1)}, bf16[2,10240,128]{2,1,0:T(8,128)(2,1)}, u32[]{:S(2)}) copy-start(bf16[2,10240,128]{2,1,0:T(8,128)(2,1)} %param.6) | copy-start | bytes 15728644

commit v3 on v2

--- a/solution.py
+++ b/solution.py
@@ -9,7 +9,7 @@
 
 BLOCK = 128
 MESH = pl.DeviceIdType.MESH
-SUB = 8
+SUB = 12
 
 
 def contract_rows(left, right):

time: 179 us -> 178 us (level)
  no operation moved by 1% of the time
where the time goes in v3:
time: 178 us
  Pallas kernels  148 us (83%)
  matrix products  26.7 us (15%)
  other arithmetic  3.08 us (2%)
    pallas_call x1, Pallas kernels, exchange(): pl.pallas_call(functools.partial(exchange_kernel, n_row, sub), out_shape=...  121 us
    pallas_call x1, Pallas kernels, project(): pl.pallas_call(functools.partial(project_kernel, n_row), out_shape=jax.Sh...  20.8 us
    dot_general x1, matrix products, contract_cols(): lax.dot_general(left, right, (((1,), (1,)), ((), ())), preferred_element_...  17.9 us
    pallas_call x1, Pallas kernels, region_rows(): pl.pallas_call(region_kernel, out_shape=jax.ShapeDtypeStruct((count, BLOC...  6.48 us
    dot_general x1, matrix products, per_device(): lax.dot_general(reflectors, eigvecs, (((1,), (0,)), ((), ())), preferred_...  4.79 us
    dot_general x1, matrix products, contract_rows(): lax.dot_general(left, right, (((0,), (0,)), ((), ())), preferred_element_...  4.06 us

profile of v3, /device:TPU:6, one launch (start us, length us, event | category | flops | bytes accessed | tf_op | source)
XLA Modules:
  0.0 178.1 jit_solution(3935012276134980721)
XLA Ops:
  0.0 0.0 copy-start.1
  0.0 0.0 copy-start
  0.0 1.4 broadcast_subtract_fusion.index_ref
  1.4 1.0 multiply_divide_fusion
  2.3 0.1 iota_compare_fusion
  2.4 4.1 %fusion.4.g_ref = f32[128,128]{1,0:T(8,128)} fusion(bf16[2,10240,128]{2,1,0:T(8,128)(2,1)} %param.6), kind=kOutput, calls=%fused_computation.5 | convolution fusion | flops 335544320 | bytes 5308416 | tf_op jit(solution)/shard_map/dot_general | solution.py:16
  6.5 0.0 copy-done.1
  6.5 0.7 broadcast_select_fusion.t_ref
  7.1 0.0 copy-done
  7.2 4.8 %fusion.2 = f32[2,128,256]{2,1,0:T(8,128)} fusion(bf16[2,10240,128]{2,1,0:T(8,128)(2,1)S(1)} %copy-done, bf16[10240,256]{1,0:T(8,128)(2,1)} %param.5), kind=kOutput, calls=%fused_computation.3 | convolution fusion | flops 1342177280 | bytes 10747904 | tf_op jit(solution)/shard_map/dot_general | solution.py:364
  11.9 20.8 %project.1.p_ref = bf16[2,128,256]{2,1,0:T(8,128)(2,1)} custom-call(f32[256,256]{1,0:T(8,128)} %bitcast.18, f32[128,128]{1,0:T(8,128)} %fusion.4.g_ref, f32[2,128,128]{2,1,0:T(8,128)} %broadcast_select_fusion.t_ref), custom_call_target="tpu_custom_call" | custom-call | tf_op jit(solution)/shard_map/project/pallas_call | solution.py:304
  32.8 6.5 %region.1 = bf16[18,128,256]{2,1,0:T(8,128)(2,1)} custom-call(s32[18]{0:T(128)} %broadcast_subtract_fusion.index_ref, bf16[2,128,256]{2,1,0:T(8,128)(2,1)} %project.1.p_ref, bf16[80,128,256]{2,1,0:T(8,128)(2,1)} %bitcast.16, bf16[2,80,128,128]{3,2,1,0:T(8,128)(2,1)} %bitcast.15), custom_call_target="tpu_custom_call" | custom-call | tf_op jit(solution)/shard_map/region/pallas_call | solution.py:347
  39.2 121.0 %exchange.1 = (bf16[2304,2048]{1,0:T(8,128)(2,1)}, bf16[1152,2048]{1,0:T(8,128)(2,1)}) custom-call(bf16[2304,256]{1,0:T(8,128)(2,1)} %bitcast.17), custom_call_target="tpu_custom_call" | custom-call | tf_op jit(solution)/shard_map/exchange/pallas_call | solution.py:203
  160.2 17.9 %fusion = f32[2304,1152]{1,0:T(8,128)} fusion(bf16[1152,2048]{1,0:T(8,128)(2,1)} %get-tuple-element.8, bf16[2304,2048]{1,0:T(8,128)(2,1)} %get-tuple-element.7, f32[2048]{0:T(1024)S(1)} %multiply_divide_fusion), kind=kOutput, calls=%fused_computation.1 | convolution fusion | flops 10885791744 | bytes 24780800 | tf_op jit(solution)/shard_map/dot_general | solution.py:22
  (1 shorter events, 0.0 us)
Async XLA Ops:
  0.0 6.5 %copy-start.1 = (f32[2,128,128]{2,1,0:T(8,128)S(1)}, f32[2,128,128]{2,1,0:T(8,128)}, u32[]{:S(2)}) copy-start(f32[2,128,128]{2,1,0:T(8,128)} %param.7) | copy-start | bytes 393220
  0.0 7.1 %copy-start = (bf16[2,10240,128]{2,1,0:T(8,128)(2,1)S(1)}, bf16[2,10240,128]{2,1,0:T(8,128)(2,1)}, u32[]{:S(2)}) copy-start(bf16[2,10240,128]{2,1,0:T(8,128)(2,1)} %param.6) | copy-start | bytes 15728644
